TPU v7x, 32 devices: a whole 2x2x4 slice. The times are simulated.
32 devices in a mesh: tm: 8 (over y, x, core), scen: 4 (over z).
Axes of the slice: x: 2, y: 2, z: 4, core: 2. Of those that a mesh axis runs over, the one named last changes fastest.
Arguments:
- closed_loop: float32 [256, 96, 96], P('tm'), may hold values from -1 to 1
- gains: float32 [256, 48, 96], P('tm'), may hold values from -0.625 to 0.625
- feedforward: float32 [256, 48], P('tm'), may hold values from -6 to 6
- drift_terms: float32 [256, 96], P('tm'), may hold values from -0.3 to 0.3
- initial_states: float32 [96, 256], P(None, ('tm', 'scen')), may hold values from -6 to 6
Outputs:
- states: float32 [256, 96, 256], P(('tm', 'scen'))
- controls: float32 [256, 48, 256], P(('tm', 'scen'))
All inputs are finite; a program needn't handle non-finite values.
Results may differ from a plain program's by a relative error of at most 0.0003.
Values sent between devices are 32-bit elements; how exact they have to be, the bound alone decides.
A program may use at most 64 MiB of HBM per device.

v0:
```python
import functools
import jax
import jax.numpy as jnp
from jax import lax
from jax.experimental import pallas as pl
from jax.experimental.pallas import tpu as pltpu
from jax.sharding import PartitionSpec as P

LANES = 128
MESH = pl.DeviceIdType.MESH
f32 = jnp.float32
bf16 = jnp.bfloat16


def up(value, unit):
    return -(-value // unit) * unit


def split(value):
    high = value.astype(bf16)
    low = (value - high.astype(f32)).astype(bf16)
    return jnp.concatenate([high, low], axis=1)


def product(left, right):
    wide = right.shape[1] // 2
    both = jnp.concatenate([right, right], axis=0)
    out = jnp.dot(left, both, preferred_element_type=f32)
    return out[:, :wide] + out[:, wide:]


def stack_rows(rows):
    high = rows.astype(bf16)
    low = (rows - high.astype(f32)).astype(bf16)
    return jnp.concatenate(
        [jnp.concatenate([high, high], axis=1), jnp.concatenate([low, low], axis=1)], axis=0
    )


def apply_rows(stacked, maps):
    out = lax.dot_general(
        stacked, maps, (((1,), (1,)), ((), ())), preferred_element_type=f32
    )
    half = out.shape[0] // 2
    return out[:half] + out[half:]


def rollout_kernel(
    n, nx, nu, tl, sl,
    a_hbm, k_hbm, ff_hbm, d_hbm, x0_hbm, states_ref, controls_ref,
    a_ref, k_ref, ff_ref, d_ref, x0_ref,
    leaf, nodes, pre, wf, w2, tile, x_send, x_all, t_send, t_recv, p_send, p_recv, send, recv,
    x_tile, u_tile, in_sem, x_ssem, x_rsem, t_ssem, t_rsem, p_ssem, p_rsem, o_ssem, o_rsem,
):
    D = tile.shape[0]
    dr = t_send.shape[0]
    rows = nx + nu
    pairs = n // 2
    me = lax.axis_index("tm")
    pair, odd = me // 2, me % 2

    loads = [
        pltpu.make_async_copy(src, dst, in_sem.at[i])
        for i, (src, dst) in enumerate(
            ((d_hbm, d_ref), (a_hbm, a_ref), (x0_hbm, x0_ref), (ff_hbm, ff_ref), (k_hbm, k_ref))
        )
    ]
    for load in loads:
        load.start()
    barrier = pltpu.get_barrier_semaphore()
    for k in range(1, n):
        pl.semaphore_signal(
            barrier, inc=1, device_id={"tm": (me + k) % n}, device_id_type=MESH
        )

    lane = lax.broadcasted_iota(jnp.int32, (D, D), 1)
    row = lax.broadcasted_iota(jnp.int32, (D, D), 0)
    corner = jnp.where((lane == nx) & (row == nx), 1.0, 0.0).astype(f32)

    tile[...] = jnp.zeros((D, D), f32)
    loads[0].wait()
    tile[0:tl, 0:nx] = d_ref[...]
    d_cols = jnp.transpose(tile[...])
    side = jnp.zeros((nx, D - nx), f32)
    side_u = jnp.zeros((nu, D - nx), f32)
    loads[1].wait()
    foot = jnp.zeros((D - nx, D), f32)

    def make_leaf(t):
        a = jnp.concatenate([jnp.concatenate([a_ref[t], side], axis=1), foot], axis=0)
        a = jnp.where(lane == nx, pltpu.roll(d_cols, nx - t, 1), a) + corner
        leaf[t, 0:D] = split(a)

    for t in range(tl):
        make_leaf(t)

    def node(level, k):
        if level == 0:
            return leaf[k, 0:D]
        return nodes[tl - 2 * (tl >> level) + k]

    levels = tl.bit_length() - 1
    root = None
    batch = 4
    for level in range(1, levels + 1):
        count = tl >> level

        for first in range(0, count, batch):
            group = range(first, min(count, first + batch))
            values = [product(node(level - 1, 2 * k + 1), node(level - 1, 2 * k)) for k in group]
            if level == levels:
                root = values[0]
                break
            for k, value in zip(group, values):
                nodes[tl - 2 * (tl >> level) + k] = split(value)
    root_split = split(root)
    t_send[...] = root[:dr]

    pl.semaphore_wait(barrier, n - 1)

    loads[2].wait()
    x_rows = jnp.concatenate([x0_ref[...], jnp.zeros((sl, D - nx), f32)], axis=1)
    x_rows = jnp.where(lax.broadcasted_iota(jnp.int32, (sl, D), 1) == nx, 1.0, x_rows)
    x_send[...] = x_rows
    x_all[me] = x_rows

    def x_copy(src, dst):
        return pltpu.make_async_remote_copy(
            src_ref=x_send, dst_ref=x_all.at[src],
            send_sem=x_ssem.at[dst], recv_sem=x_rsem.at[src],
            device_id={"tm": dst}, device_id_type=MESH,
        )

    t_copy = pltpu.make_async_remote_copy(
        src_ref=t_send, dst_ref=t_recv, send_sem=t_ssem, recv_sem=t_rsem,
        device_id={"tm": me + 1 - 2 * odd}, device_id_type=MESH,
    )

    @pl.when(odd == 0)
    def _():
        t_copy.start()

    for k in range(1, n):
        x_copy(me, (me + k) % n).start()

    loads[3].wait()
    tile[...] = jnp.zeros((D, D), f32)
    tile[0:tl, 0:nu] = ff_ref[...]
    f_cols = jnp.transpose(tile[...])[:nu]
    lane_u = lax.broadcasted_iota(jnp.int32, (nu, D), 1)
    loads[4].wait()

    def make_gain(t):
        g = -jnp.concatenate([k_ref[t], side_u], axis=1)
        g = jnp.where(lane_u == nx, pltpu.roll(f_cols, nx - t, 1), g)
        leaf[t, D : D + nu] = split(g)

    for t in range(tl):
        make_gain(t)

    eye = jnp.where((lane == row) & (lane <= nx), 1.0, 0.0).astype(f32)
    pre[0] = split(eye)
    wf[pl.ds(0, nx, stride=tl), :] = eye[:nx]

    def put_pre(t, value):
        pre[t] = split(value)
        wf[pl.ds(t, nx, stride=tl), :] = value[:nx]

    def p_copy(src_pair, dst):
        return pltpu.make_async_remote_copy(
            src_ref=p_send, dst_ref=p_recv.at[src_pair],
            send_sem=p_ssem.at[dst], recv_sem=p_rsem.at[src_pair],
            device_id={"tm": dst}, device_id_type=MESH,
        )

    pad_rows = jnp.zeros((D - dr, D), f32)

    def full(value):
        return split(jnp.concatenate([value, pad_rows], axis=0))

    def pass_pair():
        @pl.when(odd == 1)
        def _():
            t_copy.wait_recv()
            p_send[...] = product(root_split, full(t_recv[...]))[:dr]

            def go(j, c):
                p_copy(pair, n + 2 * pair + 1 - j).start()
                return c

            lax.fori_loop(2 * pair + 2, n, go, 0)

    for level in range(levels - 1, 0, -1):
        size = 1 << level
        put_first = nodes[tl - 2 * (tl >> level)]
        pre[size] = put_first
        wf[pl.ds(size, nx, stride=tl), :] = (
            put_first[:nx, :D].astype(f32) + put_first[:nx, D:].astype(f32)
        )
        count = (tl >> (level + 1)) - 1

        for first in range(0, count, batch):
            group = [2 * (j + 1) for j in range(first, min(count, first + batch))]
            values = [product(node(level, k), pre[size * k]) for k in group]
            for k, value in zip(group, values):
                put_pre(size * (k + 1), value)
        if level == min(2, levels - 1):
            pass_pair()

    for first in range(0, tl, 2 * batch):
        group = range(first, min(tl, first + 2 * batch), 2)
        values = [product(leaf[t], pre[t]) for t in group]
        for t, value in zip(group, values):
            put_pre(t + 1, value[:D])
            wf[pl.ds(nx * tl + t, nu, stride=tl), :] = value[D:]
        values = [product(leaf[t + 1, D : D + nu], pre[t + 1]) for t in group]
        for t, value in zip(group, values):
            wf[pl.ds(nx * tl + t + 1, nu, stride=tl), :] = value

    width = 4 * LANES

    def halve(j, c):
        part = pl.ds(pl.multiple_of(j * width, width), width)
        w2[part, :] = split(wf[part, :])
        return c

    lax.fori_loop(0, rows * tl // width, halve, 0)

    for k in range(1, n):
        x_copy((me + k) % n, me).wait_recv()
    entry = jnp.concatenate([x_all[k] for k in range(n)], axis=0)

    def chain(p, entry):
        p_copy(p, me).wait_recv()
        return apply_rows(stack_rows(entry), full(p_recv[p]))

    entry = lax.fori_loop(0, pair, chain, entry)
    partner = jnp.where(odd == 1, t_recv[...], eye[:dr])
    entry = apply_rows(stack_rows(entry), full(partner))
    stacked = stack_rows(entry)

    chunks = o_ssem.shape[1]
    span = rows * tl // chunks

    def o_copy(src, dst, c):
        return pltpu.make_async_remote_copy(
            src_ref=send.at[dst, :, pl.ds(c * span, span)],
            dst_ref=recv.at[src, :, pl.ds(c * span, span)],
            send_sem=o_ssem.at[dst, c], recv_sem=o_rsem.at[src, c],
            device_id={"tm": dst}, device_id_type=MESH,
        )

    for c in range(chunks):
        for start in range(c * span, (c + 1) * span, width):
            part = apply_rows(stacked, w2[start : start + width])
            for d in range(n):
                send[d, :, start : start + width] = part[d * sl : (d + 1) * sl]
        for k in range(1, n):
            o_copy(me, (me + k) % n, c).start()
    recv[me] = send[me]

    for k in range(1, n):
        x_copy(me, (me + k) % n).wait_send()

    @pl.when(odd == 0)
    def _():
        t_copy.wait_send()

    @pl.when(odd == 1)
    def _():
        def done(dst, c):
            p_copy(pair, dst).wait_send()
            return c

        lax.fori_loop(2 * pair + 2, n, done, 0)

    group = LANES // tl
    place = lax.broadcasted_iota(jnp.int32, (sl, LANES), 1) // tl
    per = LANES // tl
    for h in range(n // group):
        for c in range(chunks):
            for b in range(group):
                src = h * group + b

                @pl.when(src != me)
                def _(src=src, c=c):
                    o_copy(src, me, c).wait_recv()

            for q in range(c * span // LANES, (c + 1) * span // LANES):
                parts = [
                    recv[h * group + b, :, q * LANES : (q + 1) * LANES] for b in range(group)
                ]
                for i in range(per):
                    value = None
                    for b in range(group):
                        shift = ((b - i) * tl) % LANES
                        moved = pltpu.roll(parts[b], shift, 1) if shift else parts[b]
                        value = moved if value is None else jnp.where(place == b, moved, value)
                    index = q * per + i
                    if index < nx:
                        x_tile[pl.ds(index, sl, stride=nx), :] = value
                    else:
                        u_tile[pl.ds(index - nx, sl, stride=nu), :] = value

        steps = slice(h * LANES, (h + 1) * LANES)
        for s in range(sl):
            states_ref[s, :, steps] = x_tile[s * nx : (s + 1) * nx]
            controls_ref[s, :, steps] = u_tile[s * nu : (s + 1) * nu]

    for c in range(chunks):
        for k in range(1, n):
            o_copy(me, (me + k) % n, c).wait_send()


def body(closed_loop, gains, feedforward, drift_terms, initial_states):
    tl, nx = closed_loop.shape[:2]
    nu = gains.shape[1]
    sl = initial_states.shape[1]
    n = lax.axis_size("tm")
    D = up(nx + 1, LANES)
    dr = up(nx + 1, 8)
    rows = nx + nu
    vmem = pl.BlockSpec(memory_space=pltpu.VMEM)
    dma = pltpu.SemaphoreType.DMA
    hbm = pl.BlockSpec(memory_space=pltpu.HBM)
    chunks = rows // nu if nx % nu == 0 and (nu * tl) % (4 * LANES) == 0 else 1
    steps = n * tl
    return pl.pallas_call(
        functools.partial(rollout_kernel, n, nx, nu, tl, sl),
        out_shape=(
            jax.ShapeDtypeStruct((sl, nx, steps), f32),
            jax.ShapeDtypeStruct((sl, nu, steps), f32),
        ),
        in_specs=[hbm] * 5,
        out_specs=(vmem, vmem),
        scratch_shapes=[
            pltpu.VMEM((tl, nx, nx), f32),
            pltpu.VMEM((tl, nu, nx), f32),
            pltpu.VMEM((tl, nu), f32),
            pltpu.VMEM((tl, nx), f32),
            pltpu.VMEM((sl, nx), f32),
            pltpu.VMEM((tl, D + nu, 2 * D), bf16),
            pltpu.VMEM((tl, D, 2 * D), bf16),
            pltpu.VMEM((tl, D, 2 * D), bf16),
            pltpu.VMEM((rows * tl, D), f32),
            pltpu.VMEM((rows * tl, 2 * D), bf16),
            pltpu.VMEM((D, D), f32),
            pltpu.VMEM((sl, D), f32),
            pltpu.VMEM((n, sl, D), f32),
            pltpu.VMEM((dr, D), f32),
            pltpu.VMEM((dr, D), f32),
            pltpu.VMEM((dr, D), f32),
            pltpu.VMEM((n // 2, dr, D), f32),
            pltpu.VMEM((n, sl, rows * tl), f32),
            pltpu.VMEM((n, sl, rows * tl), f32),
            pltpu.VMEM((sl * nx, LANES), f32),
            pltpu.VMEM((sl * nu, LANES), f32),
            dma((5,)),
            dma((n,)), dma((n,)), dma, dma, dma((n,)), dma((n // 2,)),
            dma((n, chunks)), dma((n, chunks)),
        ],
        compiler_params=pltpu.CompilerParams(
            collective_id=0, has_side_effects=True, vmem_limit_bytes=48 * 2**20
        ),
    )(
        *(
            pltpu.with_memory_space_constraint(value, pltpu.HBM)
            for value in (closed_loop, gains, feedforward, drift_terms, initial_states.T)
        )
    )


def solution(mesh):
    return jax.shard_map(
        body,
        mesh=mesh,
        in_specs=(
            P("tm", None, None),
            P("tm", None, None),
            P("tm", None),
            P("tm", None),
            P(None, ("tm", "scen")),
        ),
        out_specs=(P(("tm", "scen"), None, None), P(("tm", "scen"), None, None)),
        check_vma=False,
    )
```

profile of v0, /device:TPU:1, one launch (start us, length us, event | category | flops | bytes accessed | tf_op | source)
XLA Modules:
  0.0 27.4 jit_solution(14575677033999296921)
XLA Ops:
  0.6 25.1 %shard_map.68 = (f32[8,96,256]{2,1,0:T(8,128)S(1)}, f32[8,48,256]{2,1,0:T(8,128)S(1)}) custom-call(f32[32,96,96]{2,1,0:T(8,128)} %a_hbm.1, f32[32,48,96]{2,1,0:T(8,128)} %k_hbm.1, f32[32,48]{1,0:T(8,128)} %ff_hbm.1, f32[32,96]{1,0:T(8,128)} %d_hbm.1, f32[8,96]{1,0:T(8,128)} %bitcast.1), custom_call_target="tpu_custom_call" | custom-call | tf_op jit(solution)/shard_map/pallas_call | solution.py:328
  25.8 0.9 %copy.9 = f32[8,96,256]{2,1,0:T(8,128)} copy(f32[8,96,256]{2,1,0:T(8,128)S(1)} %get-tuple-element.4) | data formatting | bytes 1572864
  26.6 0.7 %copy.10 = f32[8,48,256]{2,1,0:T(8,128)} copy(f32[8,48,256]{2,1,0:T(8,128)S(1)} %get-tuple-element.5) | data formatting | bytes 786432
where the time goes:
time: 27.8 us; the launch traced here: 27.4 us
  Pallas kernels  25.1 us (90%)
  local copies, waits for them, and re-layouts  1.63 us (6%)
  between operations  0.64 us (2%)
    pallas_call x1, Pallas kernels, body(): pl.pallas_call(functools.partial(rollout_kernel, n, nx, nu, tl, sl), out_...  25.1 us
    unnamed x2, local copies, waits for them, and re-layouts  1.63 us

commit v1 on v0

--- a/solution.py
+++ b/solution.py
@@ -47,10 +47,10 @@
 
 def rollout_kernel(
     n, nx, nu, tl, sl,
-    a_hbm, k_hbm, ff_hbm, d_hbm, x0_hbm, states_ref, controls_ref,
+    a_hbm, k_hbm, ff_hbm, d_hbm, x0_hbm, x_tile, u_tile,
     a_ref, k_ref, ff_ref, d_ref, x0_ref,
-    leaf, nodes, pre, wf, w2, tile, x_send, x_all, t_send, t_recv, p_send, p_recv, send, recv,
-    x_tile, u_tile, in_sem, x_ssem, x_rsem, t_ssem, t_rsem, p_ssem, p_rsem, o_ssem, o_rsem,
+    leaf, nodes, pre, wf, tile, x_send, x_all, t_send, t_recv, p_send, p_recv, send, recv,
+    in_sem, x_ssem, x_rsem, t_ssem, t_rsem, p_ssem, p_rsem, o_ssem, o_rsem,
 ):
     D = tile.shape[0]
     dr = t_send.shape[0]
@@ -217,15 +217,6 @@
         for t, value in zip(group, values):
             wf[pl.ds(nx * tl + t + 1, nu, stride=tl), :] = value
 
-    width = 4 * LANES
-
-    def halve(j, c):
-        part = pl.ds(pl.multiple_of(j * width, width), width)
-        w2[part, :] = split(wf[part, :])
-        return c
-
-    lax.fori_loop(0, rows * tl // width, halve, 0)
-
     for k in range(1, n):
         x_copy((me + k) % n, me).wait_recv()
     entry = jnp.concatenate([x_all[k] for k in range(n)], axis=0)
@@ -251,13 +242,13 @@
         )
 
     for c in range(chunks):
-        for start in range(c * span, (c + 1) * span, width):
-            part = apply_rows(stacked, w2[start : start + width])
-            for d in range(n):
-                send[d, :, start : start + width] = part[d * sl : (d + 1) * sl]
+        here = slice(c * span, (c + 1) * span)
+        part = apply_rows(stacked, split(wf[here, :]))
+        for d in range(n):
+            send[d, :, here] = part[d * sl : (d + 1) * sl]
+        recv[me, :, here] = send[me, :, here]
         for k in range(1, n):
             o_copy(me, (me + k) % n, c).start()
-    recv[me] = send[me]
 
     for k in range(1, n):
         x_copy(me, (me + k) % n).wait_send()
@@ -277,8 +268,8 @@
     group = LANES // tl
     place = lax.broadcasted_iota(jnp.int32, (sl, LANES), 1) // tl
     per = LANES // tl
-    for h in range(n // group):
-        for c in range(chunks):
+    for c in range(chunks):
+        for h in range(n // group):
             for b in range(group):
                 src = h * group + b
 
@@ -298,18 +289,27 @@
                         value = moved if value is None else jnp.where(place == b, moved, value)
                     index = q * per + i
                     if index < nx:
-                        x_tile[pl.ds(index, sl, stride=nx), :] = value
+                        x_tile[h, pl.ds(index, sl, stride=nx), :] = value
                     else:
-                        u_tile[pl.ds(index - nx, sl, stride=nu), :] = value
-
-        steps = slice(h * LANES, (h + 1) * LANES)
-        for s in range(sl):
-            states_ref[s, :, steps] = x_tile[s * nx : (s + 1) * nx]
-            controls_ref[s, :, steps] = u_tile[s * nu : (s + 1) * nu]
+                        u_tile[h, pl.ds(index - nx, sl, stride=nu), :] = value
 
     for c in range(chunks):
         for k in range(1, n):
             o_copy(me, (me + k) % n, c).wait_send()
+
+
+def store_kernel(halves, x_ref, u_ref, states_hbm, controls_hbm, sem):
+    copies = [
+        pltpu.make_async_copy(
+            src.at[h], dst.at[:, :, pl.ds(h * LANES, LANES)], sem.at[i, h]
+        )
+        for i, (src, dst) in enumerate(((x_ref, states_hbm), (u_ref, controls_hbm)))
+        for h in range(halves)
+    ]
+    for copy in copies:
+        copy.start()
+    for copy in copies:
+        copy.wait()
 
 
 def body(closed_loop, gains, feedforward, drift_terms, initial_states):
@@ -323,13 +323,14 @@
     vmem = pl.BlockSpec(memory_space=pltpu.VMEM)
     dma = pltpu.SemaphoreType.DMA
     hbm = pl.BlockSpec(memory_space=pltpu.HBM)
-    chunks = rows // nu if nx % nu == 0 and (nu * tl) % (4 * LANES) == 0 else 1
+    chunks = rows * tl // (4 * LANES) if rows * tl % (4 * LANES) == 0 else 1
     steps = n * tl
-    return pl.pallas_call(
+    halves = steps // LANES
+    x_tile, u_tile = pl.pallas_call(
         functools.partial(rollout_kernel, n, nx, nu, tl, sl),
         out_shape=(
-            jax.ShapeDtypeStruct((sl, nx, steps), f32),
-            jax.ShapeDtypeStruct((sl, nu, steps), f32),
+            jax.ShapeDtypeStruct((halves, sl * nx, LANES), f32),
+            jax.ShapeDtypeStruct((halves, sl * nu, LANES), f32),
         ),
         in_specs=[hbm] * 5,
         out_specs=(vmem, vmem),
@@ -343,7 +344,6 @@
             pltpu.VMEM((tl, D, 2 * D), bf16),
             pltpu.VMEM((tl, D, 2 * D), bf16),
             pltpu.VMEM((rows * tl, D), f32),
-            pltpu.VMEM((rows * tl, 2 * D), bf16),
             pltpu.VMEM((D, D), f32),
             pltpu.VMEM((sl, D), f32),
             pltpu.VMEM((n, sl, D), f32),
@@ -353,8 +353,6 @@
             pltpu.VMEM((n // 2, dr, D), f32),
             pltpu.VMEM((n, sl, rows * tl), f32),
             pltpu.VMEM((n, sl, rows * tl), f32),
-            pltpu.VMEM((sl * nx, LANES), f32),
-            pltpu.VMEM((sl * nu, LANES), f32),
             dma((5,)),
             dma((n,)), dma((n,)), dma, dma, dma((n,)), dma((n // 2,)),
             dma((n, chunks)), dma((n, chunks)),
@@ -368,6 +366,17 @@
             for value in (closed_loop, gains, feedforward, drift_terms, initial_states.T)
         )
     )
+    return pl.pallas_call(
+        functools.partial(store_kernel, halves),
+        out_shape=(
+            jax.ShapeDtypeStruct((sl, nx, steps), f32),
+            jax.ShapeDtypeStruct((sl, nu, steps), f32),
+        ),
+        in_specs=[vmem] * 2,
+        out_specs=(hbm, hbm),
+        scratch_shapes=[dma((2, halves))],
+        compiler_params=pltpu.CompilerParams(vmem_limit_bytes=2**20),
+    )(x_tile.reshape(halves, sl, nx, LANES), u_tile.reshape(halves, sl, nu, LANES))
 
 
 def solution(mesh):

time: 27.8 us -> 28.1 us (1.011)
  the two profiles are of different devices: /device:TPU:1 before, /device:TPU:0 now
where the time goes in v1:
time: 28.1 us; the launch traced here: 27.9 us
  Pallas kernels  27.2 us (97%)
  between operations  0.64 us (2%)
    pallas_call x1, Pallas kernels, body(): pl.pallas_call(functools.partial(rollout_kernel, n, nx, nu, tl, sl), out_...  26.2 us
    pallas_call x1, Pallas kernels, body(): pl.pallas_call(functools.partial(store_kernel, halves), out_shape=(jax.Sh...  1.04 us

profile of v1, /device:TPU:0, one launch (start us, length us, event | category | flops | bytes accessed | tf_op | source)
XLA Modules:
  0.0 27.9 jit_solution(3744788782145899119)
XLA Ops:
  0.6 26.2 %shard_map.68 = (f32[2,768,128]{2,1,0:T(8,128)S(1)}, f32[2,384,128]{2,1,0:T(8,128)S(1)}) custom-call(f32[32,96,96]{2,1,0:T(8,128)} %a_hbm.1, f32[32,48,96]{2,1,0:T(8,128)} %k_hbm.1, f32[32,48]{1,0:T(8,128)} %ff_hbm.1, f32[32,96]{1,0:T(8,128)} %d_hbm.1, f32[8,96]{1,0:T(8,128)} %bitcast.5), custom_call_target="tpu_custom_call" | custom-call | tf_op jit(solution)/shard_map/pallas_call | solution.py:329
  26.8 1.0 %shard_map.69 = (f32[8,96,256]{2,1,0:T(8,128)}, f32[8,48,256]{2,1,0:T(8,128)}) custom-call(f32[2,8,96,128]{3,2,1,0:T(8,128)S(1)} %bitcast.3, f32[2,8,48,128]{3,2,1,0:T(8,128)S(1)} %bitcast.4), custom_call_target="tpu_custom_call" | custom-call | tf_op jit(solution)/shard_map/pallas_call | solution.py:369

commit v2 on v1

--- a/solution.py
+++ b/solution.py
@@ -7,9 +7,56 @@
 from jax.sharding import PartitionSpec as P
 
 LANES = 128
+SIZES = (3, 3)
+SOON = 7
+PIECES = 1
+BATCH = 4
+WIDE = 8
 MESH = pl.DeviceIdType.MESH
 f32 = jnp.float32
 bf16 = jnp.bfloat16
+
+
+def spans(total, unit):
+    left, edges = total // unit, [0]
+    for size in SIZES:
+        if size < left:
+            left -= size
+            edges.append(edges[-1] + size * unit)
+    return list(zip(edges, edges[1:] + [total]))
+
+
+def order(me, n):
+    if n != 8:
+        return [(me + k) % n for k in range(1, n)]
+    table = []
+    for m in range(n):
+        pair = m // 2
+        first, last = {0: (2, 1), 1: (3, 2), 2: (3, 1), 3: (1, 2)}[pair]
+        rest = [2 * first, 2 * first + 1] + [1] * (pair > 0) + [2 * last, 2 * last + 1]
+        row = [0] * (pair > 0) + [m + 1 - 2 * (m % 2)] + rest
+        table.append(row + [6, 7] * (pair == 0))
+    return [
+        functools.reduce(lambda acc, m: jnp.where(me == m, table[m][k], acc), range(n), 0)
+        for k in range(n - 1)
+    ]
+
+
+def exchange(values, tl):
+    group = len(values)
+    lane = lax.broadcasted_iota(jnp.int32, values[0].shape, 1) // tl
+    gap = group // 2
+    while gap:
+        low = (lane // gap) % 2 == 0
+        out = list(values)
+        for i in range(group):
+            if (i // gap) % 2 == 0:
+                a, b = values[i], values[i + gap]
+                out[i] = jnp.where(low, a, pltpu.roll(b, gap * tl, 1))
+                out[i + gap] = jnp.where(low, pltpu.roll(a, LANES - gap * tl, 1), b)
+        values = out
+        gap //= 2
+    return values
 
 
 def up(value, unit):
@@ -49,8 +96,8 @@
     n, nx, nu, tl, sl,
     a_hbm, k_hbm, ff_hbm, d_hbm, x0_hbm, x_tile, u_tile,
     a_ref, k_ref, ff_ref, d_ref, x0_ref,
-    leaf, nodes, pre, wf, tile, x_send, x_all, t_send, t_recv, p_send, p_recv, send, recv,
-    in_sem, x_ssem, x_rsem, t_ssem, t_rsem, p_ssem, p_rsem, o_ssem, o_rsem,
+    leaf, nodes, pre, wf, tile, x_send, x_all, t_send, t_recv, p_send, m_recv, e_send, e_recv, send, recv,
+    in_sem, x_ssem, x_rsem, t_ssem, t_rsem, e_ssem, e_rsem, m_ssem, m_rsem, p_ssem, o_ssem, o_rsem,
 ):
     D = tile.shape[0]
     dr = t_send.shape[0]
@@ -59,14 +106,20 @@
     me = lax.axis_index("tm")
     pair, odd = me // 2, me % 2
 
-    loads = [
-        pltpu.make_async_copy(src, dst, in_sem.at[i])
-        for i, (src, dst) in enumerate(
-            ((d_hbm, d_ref), (a_hbm, a_ref), (x0_hbm, x0_ref), (ff_hbm, ff_ref), (k_hbm, k_ref))
-        )
+    pieces = PIECES if tl % PIECES == 0 else 1
+    some = tl // pieces
+
+    def load(src, dst, i):
+        return pltpu.make_async_copy(src, dst, in_sem.at[i])
+
+    a_loads = [
+        load(a_hbm.at[pl.ds(i * some, some)], a_ref.at[pl.ds(i * some, some)], 4 + i)
+        for i in range(pieces)
     ]
-    for load in loads:
-        load.start()
+    d_load, x_load = load(d_hbm, d_ref, 0), load(x0_hbm, x0_ref, 1)
+    f_load, k_load = load(ff_hbm, ff_ref, 2), load(k_hbm, k_ref, 3)
+    for copy in (d_load, *a_loads, x_load, f_load):
+        copy.start()
     barrier = pltpu.get_barrier_semaphore()
     for k in range(1, n):
         pl.semaphore_signal(
@@ -78,12 +131,11 @@
     corner = jnp.where((lane == nx) & (row == nx), 1.0, 0.0).astype(f32)
 
     tile[...] = jnp.zeros((D, D), f32)
-    loads[0].wait()
+    d_load.wait()
     tile[0:tl, 0:nx] = d_ref[...]
     d_cols = jnp.transpose(tile[...])
     side = jnp.zeros((nx, D - nx), f32)
     side_u = jnp.zeros((nu, D - nx), f32)
-    loads[1].wait()
     foot = jnp.zeros((D - nx, D), f32)
 
     def make_leaf(t):
@@ -91,9 +143,6 @@
         a = jnp.where(lane == nx, pltpu.roll(d_cols, nx - t, 1), a) + corner
         leaf[t, 0:D] = split(a)
 
-    for t in range(tl):
-        make_leaf(t)
-
     def node(level, k):
         if level == 0:
             return leaf[k, 0:D]
@@ -101,54 +150,78 @@
 
     levels = tl.bit_length() - 1
     root = None
-    batch = 4
-    for level in range(1, levels + 1):
-        count = tl >> level
-
-        for first in range(0, count, batch):
-            group = range(first, min(count, first + batch))
+    batch = BATCH
+
+    def climb(level, first, last):
+        for start in range(first, last, batch):
+            group = range(start, min(last, start + batch))
             values = [product(node(level - 1, 2 * k + 1), node(level - 1, 2 * k)) for k in group]
             if level == levels:
-                root = values[0]
-                break
+                return values[0]
             for k, value in zip(group, values):
                 nodes[tl - 2 * (tl >> level) + k] = split(value)
+
+    for i, copy in enumerate(a_loads):
+        copy.wait()
+        if i == pieces - 1:
+            k_load.start()
+        for t in range(i * some, (i + 1) * some):
+            make_leaf(t)
+        if some % 2 == 0:
+            root = climb(1, i * some // 2, (i + 1) * some // 2)
+    for level in range(1 if some % 2 else 2, levels + 1):
+        root = climb(level, 0, tl >> level)
     root_split = split(root)
     t_send[...] = root[:dr]
 
     pl.semaphore_wait(barrier, n - 1)
 
-    loads[2].wait()
+    x_load.wait()
     x_rows = jnp.concatenate([x0_ref[...], jnp.zeros((sl, D - nx), f32)], axis=1)
     x_rows = jnp.where(lax.broadcasted_iota(jnp.int32, (sl, D), 1) == nx, 1.0, x_rows)
     x_send[...] = x_rows
     x_all[me] = x_rows
 
-    def x_copy(src, dst):
+    def x_copy(src, k):
         return pltpu.make_async_remote_copy(
             src_ref=x_send, dst_ref=x_all.at[src],
-            send_sem=x_ssem.at[dst], recv_sem=x_rsem.at[src],
-            device_id={"tm": dst}, device_id_type=MESH,
-        )
-
-    t_copy = pltpu.make_async_remote_copy(
-        src_ref=t_send, dst_ref=t_recv, send_sem=t_ssem, recv_sem=t_rsem,
-        device_id={"tm": me + 1 - 2 * odd}, device_id_type=MESH,
-    )
+            send_sem=x_ssem.at[k], recv_sem=x_rsem.at[src],
+            device_id={"tm": 2 * ((pair + k) % pairs) + 1}, device_id_type=MESH,
+        )
+
+    def to_partner(src, dst, ssem, rsem):
+        return pltpu.make_async_remote_copy(
+            src_ref=src, dst_ref=dst, send_sem=ssem, recv_sem=rsem,
+            device_id={"tm": me + 1 - 2 * odd}, device_id_type=MESH,
+        )
+
+    t_copy = to_partner(t_send, t_recv, t_ssem, t_rsem)
+    e_copy = to_partner(e_send, e_recv, e_ssem, e_rsem)
+    def m_copy(src, slot, dst, ssem):
+        return pltpu.make_async_remote_copy(
+            src_ref=src, dst_ref=m_recv.at[slot], send_sem=ssem, recv_sem=m_rsem.at[slot],
+            device_id={"tm": 2 * dst + 1}, device_id_type=MESH,
+        )
+
+    def go(q, c):
+        m_copy(t_send, me, q, m_ssem.at[q]).start()
+        return c
+
+    lax.fori_loop(pair + 1, pairs - 1, go, 0)
+    t_copy.start()
+    for k in range(1, pairs):
+        x_copy(me, k).start()
 
     @pl.when(odd == 0)
     def _():
-        t_copy.start()
-
-    for k in range(1, n):
-        x_copy(me, (me + k) % n).start()
-
-    loads[3].wait()
+        x_copy(me, 0).start()
+
+    f_load.wait()
     tile[...] = jnp.zeros((D, D), f32)
     tile[0:tl, 0:nu] = ff_ref[...]
     f_cols = jnp.transpose(tile[...])[:nu]
     lane_u = lax.broadcasted_iota(jnp.int32, (nu, D), 1)
-    loads[4].wait()
+    k_load.wait()
 
     def make_gain(t):
         g = -jnp.concatenate([k_ref[t], side_u], axis=1)
@@ -166,29 +239,24 @@
         pre[t] = split(value)
         wf[pl.ds(t, nx, stride=tl), :] = value[:nx]
 
-    def p_copy(src_pair, dst):
-        return pltpu.make_async_remote_copy(
-            src_ref=p_send, dst_ref=p_recv.at[src_pair],
-            send_sem=p_ssem.at[dst], recv_sem=p_rsem.at[src_pair],
-            device_id={"tm": dst}, device_id_type=MESH,
-        )
-
-    pad_rows = jnp.zeros((D - dr, D), f32)
+    pad_rows = corner[dr:]
 
     def full(value):
         return split(jnp.concatenate([value, pad_rows], axis=0))
 
+    passes = (odd == 0) & (pair + 1 < pairs)
+    p_copy = m_copy(p_send, pair, pairs - 1, p_ssem)
+
     def pass_pair():
-        @pl.when(odd == 1)
+        @pl.when(passes)
         def _():
             t_copy.wait_recv()
-            p_send[...] = product(root_split, full(t_recv[...]))[:dr]
-
-            def go(j, c):
-                p_copy(pair, n + 2 * pair + 1 - j).start()
-                return c
-
-            lax.fori_loop(2 * pair + 2, n, go, 0)
+            p_send[...] = product(full(t_recv[...]), root_split)[:dr]
+            p_copy.start()
+
+        @pl.when((odd == 0) & (pair + 1 == pairs))
+        def _():
+            t_copy.wait_recv()
 
     for level in range(levels - 1, 0, -1):
         size = 1 << level
@@ -207,8 +275,8 @@
         if level == min(2, levels - 1):
             pass_pair()
 
-    for first in range(0, tl, 2 * batch):
-        group = range(first, min(tl, first + 2 * batch), 2)
+    for first in range(0, tl, 2 * WIDE):
+        group = range(first, min(tl, first + 2 * WIDE), 2)
         values = [product(leaf[t], pre[t]) for t in group]
         for t, value in zip(group, values):
             put_pre(t + 1, value[:D])
@@ -217,58 +285,80 @@
         for t, value in zip(group, values):
             wf[pl.ds(nx * tl + t + 1, nu, stride=tl), :] = value
 
-    for k in range(1, n):
-        x_copy((me + k) % n, me).wait_recv()
-    entry = jnp.concatenate([x_all[k] for k in range(n)], axis=0)
-
-    def chain(p, entry):
-        p_copy(p, me).wait_recv()
-        return apply_rows(stack_rows(entry), full(p_recv[p]))
-
-    entry = lax.fori_loop(0, pair, chain, entry)
-    partner = jnp.where(odd == 1, t_recv[...], eye[:dr])
-    entry = apply_rows(stack_rows(entry), full(partner))
+    @pl.when(odd == 1)
+    def _():
+        for k in range(1, n):
+            x_copy((me + k) % n, 0).wait_recv()
+        entry = jnp.concatenate([x_all[k] for k in range(n)], axis=0)
+
+        def chain(k, entry):
+            m_copy(t_send, k, pair, p_ssem).wait_recv()
+            return apply_rows(stack_rows(entry), full(m_recv[k]))
+
+        count = jnp.where(pair == pairs - 1, pair, 2 * pair)
+        entry = lax.fori_loop(0, count, chain, entry)
+        e_send[...] = entry
+        e_copy.start()
+        t_copy.wait_recv()
+        e_recv[...] = apply_rows(stack_rows(entry), full(t_recv[...]))
+
+    @pl.when(odd == 0)
+    def _():
+        e_copy.wait_recv()
+
+    entry = e_recv[...]
     stacked = stack_rows(entry)
 
-    chunks = o_ssem.shape[1]
-    span = rows * tl // chunks
+    chunks = spans(rows * tl, 4 * LANES)
 
     def o_copy(src, dst, c):
+        start, stop = chunks[c]
+        part = pl.ds(start, stop - start)
         return pltpu.make_async_remote_copy(
-            src_ref=send.at[dst, :, pl.ds(c * span, span)],
-            dst_ref=recv.at[src, :, pl.ds(c * span, span)],
+            src_ref=send.at[dst, :, part], dst_ref=recv.at[src, :, part],
             send_sem=o_ssem.at[dst, c], recv_sem=o_rsem.at[src, c],
             device_id={"tm": dst}, device_id_type=MESH,
         )
 
-    for c in range(chunks):
-        here = slice(c * span, (c + 1) * span)
-        part = apply_rows(stacked, split(wf[here, :]))
-        for d in range(n):
-            send[d, :, here] = part[d * sl : (d + 1) * sl]
-        recv[me, :, here] = send[me, :, here]
-        for k in range(1, n):
-            o_copy(me, (me + k) % n, c).start()
-
-    for k in range(1, n):
-        x_copy(me, (me + k) % n).wait_send()
+    peers = order(me, n)
+    soon = SOON
+    for c, (start, stop) in enumerate(chunks):
+        for first in range(start, stop, 4 * LANES):
+            here = slice(first, first + 4 * LANES)
+            part = apply_rows(stacked, split(wf[here, :]))
+            for d in range(n):
+                send[d, :, here] = part[d * sl : (d + 1) * sl]
+        recv[me, :, start:stop] = send[me, :, start:stop]
+        for dst in peers[:soon]:
+            o_copy(me, dst, c).start()
+    for dst in peers[soon:]:
+        for c in range(len(chunks)):
+            o_copy(me, dst, c).start()
+
+    t_copy.wait_send()
+    for k in range(1, pairs):
+        x_copy(me, k).wait_send()
 
     @pl.when(odd == 0)
     def _():
-        t_copy.wait_send()
+        x_copy(me, 0).wait_send()
+
+    def done(q, c):
+        m_copy(t_send, me, q, m_ssem.at[q]).wait_send()
+        return c
+
+    lax.fori_loop(pair + 1, pairs - 1, done, 0)
+
+    @pl.when(passes)
+    def _():
+        p_copy.wait_send()
 
     @pl.when(odd == 1)
     def _():
-        def done(dst, c):
-            p_copy(pair, dst).wait_send()
-            return c
-
-        lax.fori_loop(2 * pair + 2, n, done, 0)
+        e_copy.wait_send()
 
     group = LANES // tl
-    place = lax.broadcasted_iota(jnp.int32, (sl, LANES), 1) // tl
-    per = LANES // tl
-    for c in range(chunks):
+    for c, (start, stop) in enumerate(chunks):
         for h in range(n // group):
             for b in range(group):
                 src = h * group + b
@@ -277,23 +367,18 @@
                 def _(src=src, c=c):
                     o_copy(src, me, c).wait_recv()
 
-            for q in range(c * span // LANES, (c + 1) * span // LANES):
-                parts = [
-                    recv[h * group + b, :, q * LANES : (q + 1) * LANES] for b in range(group)
-                ]
-                for i in range(per):
-                    value = None
-                    for b in range(group):
-                        shift = ((b - i) * tl) % LANES
-                        moved = pltpu.roll(parts[b], shift, 1) if shift else parts[b]
-                        value = moved if value is None else jnp.where(place == b, moved, value)
-                    index = q * per + i
+            for q in range(start // LANES, stop // LANES):
+                values = exchange(
+                    [recv[h * group + b, :, q * LANES : (q + 1) * LANES] for b in range(group)], tl
+                )
+                for i, value in enumerate(values):
+                    index = q * group + i
                     if index < nx:
                         x_tile[h, pl.ds(index, sl, stride=nx), :] = value
                     else:
                         u_tile[h, pl.ds(index - nx, sl, stride=nu), :] = value
 
-    for c in range(chunks):
+    for c in range(len(chunks)):
         for k in range(1, n):
             o_copy(me, (me + k) % n, c).wait_send()
 
@@ -318,12 +403,12 @@
     sl = initial_states.shape[1]
     n = lax.axis_size("tm")
     D = up(nx + 1, LANES)
-    dr = up(nx + 1, 8)
+    dr = up(nx, 8)
     rows = nx + nu
     vmem = pl.BlockSpec(memory_space=pltpu.VMEM)
     dma = pltpu.SemaphoreType.DMA
     hbm = pl.BlockSpec(memory_space=pltpu.HBM)
-    chunks = rows * tl // (4 * LANES) if rows * tl % (4 * LANES) == 0 else 1
+    chunks = len(spans(rows * tl, 4 * LANES))
     steps = n * tl
     halves = steps // LANES
     x_tile, u_tile = pl.pallas_call(
@@ -350,11 +435,14 @@
             pltpu.VMEM((dr, D), f32),
             pltpu.VMEM((dr, D), f32),
             pltpu.VMEM((dr, D), f32),
-            pltpu.VMEM((n // 2, dr, D), f32),
+            pltpu.VMEM((n, dr, D), f32),
+            pltpu.VMEM((n * sl, D), f32),
+            pltpu.VMEM((n * sl, D), f32),
             pltpu.VMEM((n, sl, rows * tl), f32),
             pltpu.VMEM((n, sl, rows * tl), f32),
-            dma((5,)),
-            dma((n,)), dma((n,)), dma, dma, dma((n,)), dma((n // 2,)),
+            dma((4 + 4,)),
+            dma((n // 2,)), dma((n,)), dma, dma, dma, dma,
+            dma((n // 2,)), dma((n,)), dma,
             dma((n, chunks)), dma((n, chunks)),
         ],
         compiler_params=pltpu.CompilerParams(

time: 28.1 us -> 26.1 us (0.929)
  the two profiles are of different devices: /device:TPU:0 before, /device:TPU:1 now
where the time goes in v2:
time: 26.1 us; the launch traced here: 25.9 us
  Pallas kernels  25.2 us (97%)
  between operations  0.64 us (2%)
    pallas_call x1, Pallas kernels, body(): pl.pallas_call(functools.partial(rollout_kernel, n, nx, nu, tl, sl), out_...  24.2 us
    pallas_call x1, Pallas kernels, body(): pl.pallas_call(functools.partial(store_kernel, halves), out_shape=(jax.Sh...  1.04 us

profile of v2, /device:TPU:1, one launch (start us, length us, event | category | flops | bytes accessed | tf_op | source)
XLA Modules:
  0.0 25.9 jit_solution(13798473787630356583)
XLA Ops:
  0.6 24.2 %shard_map.68 = (f32[2,768,128]{2,1,0:T(8,128)S(1)}, f32[2,384,128]{2,1,0:T(8,128)S(1)}) custom-call(f32[32,96,96]{2,1,0:T(8,128)} %a_hbm.1, f32[32,48,96]{2,1,0:T(8,128)} %k_hbm.1, f32[32,48]{1,0:T(8,128)} %ff_hbm.1, f32[32,96]{1,0:T(8,128)} %d_hbm.1, f32[8,96]{1,0:T(8,128)} %bitcast.5), custom_call_target="tpu_custom_call" | custom-call | tf_op jit(solution)/shard_map/pallas_call | solution.py:414
  24.8 1.0 %shard_map.69 = (f32[8,96,256]{2,1,0:T(8,128)}, f32[8,48,256]{2,1,0:T(8,128)}) custom-call(f32[2,8,96,128]{3,2,1,0:T(8,128)S(1)} %bitcast.3, f32[2,8,48,128]{3,2,1,0:T(8,128)S(1)} %bitcast.4), custom_call_target="tpu_custom_call" | custom-call | tf_op jit(solution)/shard_map/pallas_call | solution.py:457

commit v3 on v2

--- a/solution.py
+++ b/solution.py
@@ -8,8 +8,6 @@
 
 LANES = 128
 SIZES = (3, 3)
-SOON = 7
-PIECES = 1
 BATCH = 4
 WIDE = 8
 MESH = pl.DeviceIdType.MESH
@@ -29,13 +27,8 @@
 def order(me, n):
     if n != 8:
         return [(me + k) % n for k in range(1, n)]
-    table = []
-    for m in range(n):
-        pair = m // 2
-        first, last = {0: (2, 1), 1: (3, 2), 2: (3, 1), 3: (1, 2)}[pair]
-        rest = [2 * first, 2 * first + 1] + [1] * (pair > 0) + [2 * last, 2 * last + 1]
-        row = [0] * (pair > 0) + [m + 1 - 2 * (m % 2)] + rest
-        table.append(row + [6, 7] * (pair == 0))
+    rows = ((1, 0, 2, 3), (0, 1, 3, 2), (0, 2, 1, 3), (0, 3, 1, 2))
+    table = [[2 * p + d if p != m // 2 else m + 1 - 2 * (m % 2) for p in rows[m // 2] for d in range(1 + (p != m // 2))] for m in range(n)]
     return [
         functools.reduce(lambda acc, m: jnp.where(me == m, table[m][k], acc), range(n), 0)
         for k in range(n - 1)
@@ -97,7 +90,7 @@
     a_hbm, k_hbm, ff_hbm, d_hbm, x0_hbm, x_tile, u_tile,
     a_ref, k_ref, ff_ref, d_ref, x0_ref,
     leaf, nodes, pre, wf, tile, x_send, x_all, t_send, t_recv, p_send, m_recv, e_send, e_recv, send, recv,
-    in_sem, x_ssem, x_rsem, t_ssem, t_rsem, e_ssem, e_rsem, m_ssem, m_rsem, p_ssem, o_ssem, o_rsem,
+    in_sem, x_ssem, x_rsem, t_ssem, t_rsem, m_ssem, m_rsem, p_ssem, o_ssem, o_rsem,
 ):
     D = tile.shape[0]
     dr = t_send.shape[0]
@@ -106,19 +99,13 @@
     me = lax.axis_index("tm")
     pair, odd = me // 2, me % 2
 
-    pieces = PIECES if tl % PIECES == 0 else 1
-    some = tl // pieces
-
     def load(src, dst, i):
         return pltpu.make_async_copy(src, dst, in_sem.at[i])
 
-    a_loads = [
-        load(a_hbm.at[pl.ds(i * some, some)], a_ref.at[pl.ds(i * some, some)], 4 + i)
-        for i in range(pieces)
-    ]
+    a_load = load(a_hbm, a_ref, 4)
     d_load, x_load = load(d_hbm, d_ref, 0), load(x0_hbm, x0_ref, 1)
     f_load, k_load = load(ff_hbm, ff_ref, 2), load(k_hbm, k_ref, 3)
-    for copy in (d_load, *a_loads, x_load, f_load):
+    for copy in (d_load, a_load, x_load, f_load):
         copy.start()
     barrier = pltpu.get_barrier_semaphore()
     for k in range(1, n):
@@ -149,7 +136,6 @@
         return nodes[tl - 2 * (tl >> level) + k]
 
     levels = tl.bit_length() - 1
-    root = None
     batch = BATCH
 
     def climb(level, first, last):
@@ -161,32 +147,50 @@
             for k, value in zip(group, values):
                 nodes[tl - 2 * (tl >> level) + k] = split(value)
 
-    for i, copy in enumerate(a_loads):
-        copy.wait()
-        if i == pieces - 1:
-            k_load.start()
-        for t in range(i * some, (i + 1) * some):
-            make_leaf(t)
-        if some % 2 == 0:
-            root = climb(1, i * some // 2, (i + 1) * some // 2)
-    for level in range(1 if some % 2 else 2, levels + 1):
+    a_load.wait()
+    k_load.start()
+    for t in range(tl):
+        make_leaf(t)
+    root = climb(1, 0, tl // 2)
+
+    def x_copy(src, k):
+        return pltpu.make_async_remote_copy(
+            src_ref=x_send, dst_ref=x_all.at[src],
+            send_sem=x_ssem, recv_sem=x_rsem,
+            device_id={"tm": 2 * ((pair + k) % pairs) + 1}, device_id_type=MESH,
+        )
+
+    def send_x():
+        pl.semaphore_wait(barrier, n - 1)
+        x_load.wait()
+        x_rows = jnp.concatenate([x0_ref[...], jnp.zeros((sl, D - nx), f32)], axis=1)
+        x_rows = jnp.where(lax.broadcasted_iota(jnp.int32, (sl, D), 1) == nx, 1.0, x_rows)
+        x_send[...] = x_rows
+        x_all[me] = x_rows
+        for k in range(1, pairs):
+            x_copy(me, k).start()
+
+        @pl.when(odd == 0)
+        def _():
+            x_copy(me, 0).start()
+
+    @pl.when(pair > 0)
+    def _():
+        send_x()
+
+    for level in range(2, levels + 1):
         root = climb(level, 0, tl >> level)
     root_split = split(root)
     t_send[...] = root[:dr]
 
-    pl.semaphore_wait(barrier, n - 1)
-
-    x_load.wait()
-    x_rows = jnp.concatenate([x0_ref[...], jnp.zeros((sl, D - nx), f32)], axis=1)
-    x_rows = jnp.where(lax.broadcasted_iota(jnp.int32, (sl, D), 1) == nx, 1.0, x_rows)
-    x_send[...] = x_rows
-    x_all[me] = x_rows
-
-    def x_copy(src, k):
-        return pltpu.make_async_remote_copy(
-            src_ref=x_send, dst_ref=x_all.at[src],
-            send_sem=x_ssem.at[k], recv_sem=x_rsem.at[src],
-            device_id={"tm": 2 * ((pair + k) % pairs) + 1}, device_id_type=MESH,
+    @pl.when(pair == 0)
+    def _():
+        send_x()
+
+    def x_wait(count):
+        return pltpu.make_async_remote_copy(
+            src_ref=x_all.at[pl.ds(0, count)], dst_ref=x_all.at[pl.ds(0, count)],
+            send_sem=x_ssem, recv_sem=x_rsem, device_id={"tm": me}, device_id_type=MESH,
         )
 
     def to_partner(src, dst, ssem, rsem):
@@ -196,25 +200,22 @@
         )
 
     t_copy = to_partner(t_send, t_recv, t_ssem, t_rsem)
-    e_copy = to_partner(e_send, e_recv, e_ssem, e_rsem)
+    e_copy = to_partner(e_send, e_recv, p_ssem, m_rsem.at[0])
     def m_copy(src, slot, dst, ssem):
         return pltpu.make_async_remote_copy(
             src_ref=src, dst_ref=m_recv.at[slot], send_sem=ssem, recv_sem=m_rsem.at[slot],
             device_id={"tm": 2 * dst + 1}, device_id_type=MESH,
         )
 
-    def go(q, c):
-        m_copy(t_send, me, q, m_ssem.at[q]).start()
+    direct = jnp.where(pair == 0, pairs, pairs - 1)
+
+    def go(j, c):
+        q = direct + pair - j
+        m_copy(t_send, me, q, m_ssem.at[q - 1]).start()
         return c
 
-    lax.fori_loop(pair + 1, pairs - 1, go, 0)
+    lax.fori_loop(pair + 1, direct, go, 0)
     t_copy.start()
-    for k in range(1, pairs):
-        x_copy(me, k).start()
-
-    @pl.when(odd == 0)
-    def _():
-        x_copy(me, 0).start()
 
     f_load.wait()
     tile[...] = jnp.zeros((D, D), f32)
@@ -244,8 +245,9 @@
     def full(value):
         return split(jnp.concatenate([value, pad_rows], axis=0))
 
-    passes = (odd == 0) & (pair + 1 < pairs)
-    p_copy = m_copy(p_send, pair, pairs - 1, p_ssem)
+    passes = (odd == 0) & (pair > 0) & (pair + 1 < pairs)
+    keeps = (odd == 0) & ((pair == 0) | (pair + 1 == pairs))
+    p_copy = m_copy(p_send, pair + 1, pairs - 1, p_ssem)
 
     def pass_pair():
         @pl.when(passes)
@@ -254,7 +256,7 @@
             p_send[...] = product(full(t_recv[...]), root_split)[:dr]
             p_copy.start()
 
-        @pl.when((odd == 0) & (pair + 1 == pairs))
+        @pl.when(keeps)
         def _():
             t_copy.wait_recv()
 
@@ -287,15 +289,14 @@
 
     @pl.when(odd == 1)
     def _():
-        for k in range(1, n):
-            x_copy((me + k) % n, 0).wait_recv()
+        x_wait(n - 1).wait_recv()
         entry = jnp.concatenate([x_all[k] for k in range(n)], axis=0)
 
         def chain(k, entry):
             m_copy(t_send, k, pair, p_ssem).wait_recv()
             return apply_rows(stack_rows(entry), full(m_recv[k]))
 
-        count = jnp.where(pair == pairs - 1, pair, 2 * pair)
+        count = jnp.where(pair == pairs - 1, min(pairs, 2 * pairs - 2), 2 * pair)
         entry = lax.fori_loop(0, count, chain, entry)
         e_send[...] = entry
         e_copy.start()
@@ -310,18 +311,25 @@
     stacked = stack_rows(entry)
 
     chunks = spans(rows * tl, 4 * LANES)
+    group = LANES // tl
 
     def o_copy(src, dst, c):
         start, stop = chunks[c]
         part = pl.ds(start, stop - start)
         return pltpu.make_async_remote_copy(
             src_ref=send.at[dst, :, part], dst_ref=recv.at[src, :, part],
-            send_sem=o_ssem.at[dst, c], recv_sem=o_rsem.at[src, c],
+            send_sem=o_ssem, recv_sem=o_rsem.at[c, src // group],
             device_id={"tm": dst}, device_id_type=MESH,
         )
 
+    def o_wait(count, start, stop, sem):
+        part = (pl.ds(0, count), slice(None), pl.ds(start, stop - start))
+        return pltpu.make_async_remote_copy(
+            src_ref=send.at[part], dst_ref=recv.at[part], send_sem=o_ssem, recv_sem=sem,
+            device_id={"tm": me}, device_id_type=MESH,
+        )
+
     peers = order(me, n)
-    soon = SOON
     for c, (start, stop) in enumerate(chunks):
         for first in range(start, stop, 4 * LANES):
             here = slice(first, first + 4 * LANES)
@@ -329,25 +337,20 @@
             for d in range(n):
                 send[d, :, here] = part[d * sl : (d + 1) * sl]
         recv[me, :, start:stop] = send[me, :, start:stop]
-        for dst in peers[:soon]:
+        for dst in peers:
             o_copy(me, dst, c).start()
-    for dst in peers[soon:]:
-        for c in range(len(chunks)):
-            o_copy(me, dst, c).start()
 
     t_copy.wait_send()
-    for k in range(1, pairs):
-        x_copy(me, k).wait_send()
 
     @pl.when(odd == 0)
     def _():
-        x_copy(me, 0).wait_send()
+        x_wait(pairs).wait_send()
 
     def done(q, c):
-        m_copy(t_send, me, q, m_ssem.at[q]).wait_send()
+        m_copy(t_send, me, q, m_ssem.at[q - 1]).wait_send()
         return c
 
-    lax.fori_loop(pair + 1, pairs - 1, done, 0)
+    lax.fori_loop(pair + 1, direct, done, 0)
 
     @pl.when(passes)
     def _():
@@ -355,17 +358,15 @@
 
     @pl.when(odd == 1)
     def _():
+        x_wait(pairs - 1).wait_send()
         e_copy.wait_send()
 
-    group = LANES // tl
     for c, (start, stop) in enumerate(chunks):
         for h in range(n // group):
-            for b in range(group):
-                src = h * group + b
-
-                @pl.when(src != me)
-                def _(src=src, c=c):
-                    o_copy(src, me, c).wait_recv()
+            for count in (group - 1, group):
+                @pl.when((me // group == h) == (count < group))
+                def _(count=count, start=start, stop=stop, c=c, h=h):
+                    o_wait(count, start, stop, o_rsem.at[c, h]).wait_recv()
 
             for q in range(start // LANES, stop // LANES):
                 values = exchange(
@@ -378,9 +379,7 @@
                     else:
                         u_tile[h, pl.ds(index - nx, sl, stride=nu), :] = value
 
-    for c in range(len(chunks)):
-        for k in range(1, n):
-            o_copy(me, (me + k) % n, c).wait_send()
+    o_wait(n - 1, 0, rows * tl, o_rsem.at[0, 0]).wait_send()
 
 
 def store_kernel(halves, x_ref, u_ref, states_hbm, controls_hbm, sem):
@@ -440,10 +439,9 @@
             pltpu.VMEM((n * sl, D), f32),
             pltpu.VMEM((n, sl, rows * tl), f32),
             pltpu.VMEM((n, sl, rows * tl), f32),
-            dma((4 + 4,)),
-            dma((n // 2,)), dma((n,)), dma, dma, dma, dma,
-            dma((n // 2,)), dma((n,)), dma,
-            dma((n, chunks)), dma((n, chunks)),
+            dma((5,)),
+            dma, dma, dma, dma, dma((max(n // 2 - 1, 1),)), dma((max(n - 2, 1),)), dma,
+            dma, dma((chunks, halves)),
         ],
         compiler_params=pltpu.CompilerParams(
             collective_id=0, has_side_effects=True, vmem_limit_bytes=48 * 2**20

time: 26.1 us -> 25.4 us (0.973)
  Pallas kernels: 25.2 us -> 24.5 us
    pallas_call x1, Pallas kernels: 24.2 us -> 23.5 us  [body(): pl.pallas_call(functools.partial(rollout_kernel, n, nx, nu, tl, sl), out_...]
where the time goes in v3:
time: 25.4 us; the launch traced here: 25.2 us
  Pallas kernels  24.5 us (96%)
  between operations  0.64 us (3%)
    pallas_call x1, Pallas kernels, body(): pl.pallas_call(functools.partial(rollout_kernel, n, nx, nu, tl, sl), out_...  23.5 us
    pallas_call x1, Pallas kernels, body(): pl.pallas_call(functools.partial(store_kernel, halves), out_shape=(jax.Sh...  1.04 us

profile of v3, /device:TPU:1, one launch (start us, length us, event | category | flops | bytes accessed | tf_op | source)
XLA Modules:
  0.0 25.2 jit_solution(11981758190986140511)
XLA Ops:
  0.6 23.5 %shard_map.68 = (f32[2,768,128]{2,1,0:T(8,128)S(1)}, f32[2,384,128]{2,1,0:T(8,128)S(1)}) custom-call(f32[32,96,96]{2,1,0:T(8,128)} %a_hbm.1, f32[32,48,96]{2,1,0:T(8,128)} %k_hbm.1, f32[32,48]{1,0:T(8,128)} %ff_hbm.1, f32[32,96]{1,0:T(8,128)} %d_hbm.1, f32[8,96]{1,0:T(8,128)} %bitcast.5), custom_call_target="tpu_custom_call" | custom-call | tf_op jit(solution)/shard_map/pallas_call | solution.py:413
  24.1 1.0 %shard_map.69 = (f32[8,96,256]{2,1,0:T(8,128)}, f32[8,48,256]{2,1,0:T(8,128)}) custom-call(f32[2,8,96,128]{3,2,1,0:T(8,128)S(1)} %bitcast.3, f32[2,8,48,128]{3,2,1,0:T(8,128)S(1)} %bitcast.4), custom_call_target="tpu_custom_call" | custom-call | tf_op jit(solution)/shard_map/pallas_call | solution.py:455

commit v4 on v3

--- a/solution.py
+++ b/solution.py
@@ -7,7 +7,7 @@
 from jax.sharding import PartitionSpec as P
 
 LANES = 128
-SIZES = (3, 3)
+SIZES = (2, 4)
 BATCH = 4
 WIDE = 8
 MESH = pl.DeviceIdType.MESH
@@ -64,7 +64,8 @@
 
 def product(left, right):
     wide = right.shape[1] // 2
-    both = jnp.concatenate([right, right], axis=0)
+    pad = jnp.zeros((wide - right.shape[0], 2 * wide), bf16)
+    both = jnp.concatenate([right, pad, right, pad], axis=0)
     out = jnp.dot(left, both, preferred_element_type=f32)
     return out[:, :wide] + out[:, wide:]
 
@@ -83,6 +84,18 @@
     )
     half = out.shape[0] // 2
     return out[:half] + out[half:]
+
+
+def advance(rows, maps):
+    wide = maps.shape[1] // 2
+    high, low = maps[:, :wide], maps[:, wide:]
+    both = jnp.concatenate(
+        [jnp.concatenate([high, high], axis=1), jnp.concatenate([low, low], axis=1)], axis=0
+    )
+    out = lax.dot_general(
+        split(rows), both, (((1,), (1,)), ((), ())), preferred_element_type=f32
+    )
+    return out[:, :wide] + out[:, wide:]
 
 
 def rollout_kernel(
@@ -93,6 +106,7 @@
     in_sem, x_ssem, x_rsem, t_ssem, t_rsem, m_ssem, m_rsem, p_ssem, o_ssem, o_rsem,
 ):
     D = tile.shape[0]
+    R = pre.shape[1]
     dr = t_send.shape[0]
     rows = nx + nu
     pairs = n // 2
@@ -120,19 +134,20 @@
     tile[...] = jnp.zeros((D, D), f32)
     d_load.wait()
     tile[0:tl, 0:nx] = d_ref[...]
-    d_cols = jnp.transpose(tile[...])
+    d_cols = jnp.transpose(tile[...])[:nx]
     side = jnp.zeros((nx, D - nx), f32)
     side_u = jnp.zeros((nu, D - nx), f32)
-    foot = jnp.zeros((D - nx, D), f32)
+    foot = split(corner[nx:R])
+    lane_x = lax.broadcasted_iota(jnp.int32, (nx, D), 1)
 
     def make_leaf(t):
-        a = jnp.concatenate([jnp.concatenate([a_ref[t], side], axis=1), foot], axis=0)
-        a = jnp.where(lane == nx, pltpu.roll(d_cols, nx - t, 1), a) + corner
-        leaf[t, 0:D] = split(a)
+        a = jnp.concatenate([a_ref[t], side], axis=1)
+        leaf[t, 0:nx] = split(jnp.where(lane_x == nx, pltpu.roll(d_cols, nx - t, 1), a))
+        leaf[t, nx:R] = foot
 
     def node(level, k):
         if level == 0:
-            return leaf[k, 0:D]
+            return leaf[k, 0:R]
         return nodes[tl - 2 * (tl >> level) + k]
 
     levels = tl.bit_length() - 1
@@ -217,23 +232,8 @@
     lax.fori_loop(pair + 1, direct, go, 0)
     t_copy.start()
 
-    f_load.wait()
-    tile[...] = jnp.zeros((D, D), f32)
-    tile[0:tl, 0:nu] = ff_ref[...]
-    f_cols = jnp.transpose(tile[...])[:nu]
-    lane_u = lax.broadcasted_iota(jnp.int32, (nu, D), 1)
-    k_load.wait()
-
-    def make_gain(t):
-        g = -jnp.concatenate([k_ref[t], side_u], axis=1)
-        g = jnp.where(lane_u == nx, pltpu.roll(f_cols, nx - t, 1), g)
-        leaf[t, D : D + nu] = split(g)
-
-    for t in range(tl):
-        make_gain(t)
-
     eye = jnp.where((lane == row) & (lane <= nx), 1.0, 0.0).astype(f32)
-    pre[0] = split(eye)
+    pre[0] = split(eye[:R])
     wf[pl.ds(0, nx, stride=tl), :] = eye[:nx]
 
     def put_pre(t, value):
@@ -253,7 +253,7 @@
         @pl.when(passes)
         def _():
             t_copy.wait_recv()
-            p_send[...] = product(full(t_recv[...]), root_split)[:dr]
+            p_send[...] = product(split(t_recv[...]), root_split)
             p_copy.start()
 
         @pl.when(keeps)
@@ -279,13 +279,32 @@
 
     for first in range(0, tl, 2 * WIDE):
         group = range(first, min(tl, first + 2 * WIDE), 2)
-        values = [product(leaf[t], pre[t]) for t in group]
+        values = [product(leaf[t, 0:R], pre[t]) for t in group]
         for t, value in zip(group, values):
-            put_pre(t + 1, value[:D])
-            wf[pl.ds(nx * tl + t, nu, stride=tl), :] = value[D:]
-        values = [product(leaf[t + 1, D : D + nu], pre[t + 1]) for t in group]
-        for t, value in zip(group, values):
-            wf[pl.ds(nx * tl + t + 1, nu, stride=tl), :] = value
+            put_pre(t + 1, value)
+
+    def make_controls():
+        f_load.wait()
+        tile[...] = jnp.zeros((D, D), f32)
+        tile[0:tl, 0:nu] = ff_ref[...]
+        f_cols = jnp.transpose(tile[...])[:nu]
+        lane_u = lax.broadcasted_iota(jnp.int32, (nu, D), 1)
+        k_load.wait()
+
+        def make_gain(t):
+            g = -jnp.concatenate([k_ref[t], side_u], axis=1)
+            g = jnp.where(lane_u == nx, pltpu.roll(f_cols, nx - t, 1), g)
+            leaf[t, R : R + nu] = split(g)
+
+        for t in range(tl):
+            make_gain(t)
+
+
+        for first in range(0, tl, WIDE):
+            group = range(first, min(tl, first + WIDE))
+            values = [product(leaf[t, R : R + nu], pre[t]) for t in group]
+            for t, value in zip(group, values):
+                wf[pl.ds(nx * tl + t, nu, stride=tl), :] = value
 
     @pl.when(odd == 1)
     def _():
@@ -294,17 +313,18 @@
 
         def chain(k, entry):
             m_copy(t_send, k, pair, p_ssem).wait_recv()
-            return apply_rows(stack_rows(entry), full(m_recv[k]))
+            return advance(entry, full(m_recv[k]))
 
         count = jnp.where(pair == pairs - 1, min(pairs, 2 * pairs - 2), 2 * pair)
         entry = lax.fori_loop(0, count, chain, entry)
         e_send[...] = entry
         e_copy.start()
         t_copy.wait_recv()
-        e_recv[...] = apply_rows(stack_rows(entry), full(t_recv[...]))
+        e_recv[...] = advance(entry, full(t_recv[...]))
 
     @pl.when(odd == 0)
     def _():
+        make_controls()
         e_copy.wait_recv()
 
     entry = e_recv[...]
@@ -330,7 +350,14 @@
         )
 
     peers = order(me, n)
+    mixed = min(c for c, (_, stop) in enumerate(chunks) if stop > nx * tl)
     for c, (start, stop) in enumerate(chunks):
+        if c == mixed:
+
+            @pl.when(odd == 1)
+            def _():
+                make_controls()
+
         for first in range(start, stop, 4 * LANES):
             here = slice(first, first + 4 * LANES)
             part = apply_rows(stacked, split(wf[here, :]))
@@ -403,6 +430,7 @@
     n = lax.axis_size("tm")
     D = up(nx + 1, LANES)
     dr = up(nx, 8)
+    R = up(nx + 1, 16)
     rows = nx + nu
     vmem = pl.BlockSpec(memory_space=pltpu.VMEM)
     dma = pltpu.SemaphoreType.DMA
@@ -424,9 +452,9 @@
             pltpu.VMEM((tl, nu), f32),
             pltpu.VMEM((tl, nx), f32),
             pltpu.VMEM((sl, nx), f32),
-            pltpu.VMEM((tl, D + nu, 2 * D), bf16),
-            pltpu.VMEM((tl, D, 2 * D), bf16),
-            pltpu.VMEM((tl, D, 2 * D), bf16),
+            pltpu.VMEM((tl, R + nu, 2 * D), bf16),
+            pltpu.VMEM((tl, R, 2 * D), bf16),
+            pltpu.VMEM((tl, R, 2 * D), bf16),
             pltpu.VMEM((rows * tl, D), f32),
             pltpu.VMEM((D, D), f32),
             pltpu.VMEM((sl, D), f32),

time: 25.4 us -> 25.3 us (level)
  no operation moved by 1% of the time
where the time goes in v4:
time: 25.3 us; the launch traced here: 25 us
  Pallas kernels  24.4 us (96%)
  between operations  0.64 us (3%)
    pallas_call x1, Pallas kernels, body(): pl.pallas_call(functools.partial(rollout_kernel, n, nx, nu, tl, sl), out_...  23.4 us
    pallas_call x1, Pallas kernels, body(): pl.pallas_call(functools.partial(store_kernel, halves), out_shape=(jax.Sh...  1.04 us

profile of v4, /device:TPU:1, one launch (start us, length us, event | category | flops | bytes accessed | tf_op | source)
XLA Modules:
  0.0 25.0 jit_solution(3622866772506719394)
XLA Ops:
  0.6 23.4 %shard_map.68 = (f32[2,768,128]{2,1,0:T(8,128)S(1)}, f32[2,384,128]{2,1,0:T(8,128)S(1)}) custom-call(f32[32,96,96]{2,1,0:T(8,128)} %a_hbm.1, f32[32,48,96]{2,1,0:T(8,128)} %k_hbm.1, f32[32,48]{1,0:T(8,128)} %ff_hbm.1, f32[32,96]{1,0:T(8,128)} %d_hbm.1, f32[8,96]{1,0:T(8,128)} %bitcast.5), custom_call_target="tpu_custom_call" | custom-call | tf_op jit(solution)/shard_map/pallas_call | solution.py:441
  24.0 1.0 %shard_map.69 = (f32[8,96,256]{2,1,0:T(8,128)}, f32[8,48,256]{2,1,0:T(8,128)}) custom-call(f32[2,8,96,128]{3,2,1,0:T(8,128)S(1)} %bitcast.3, f32[2,8,48,128]{3,2,1,0:T(8,128)S(1)} %bitcast.4), custom_call_target="tpu_custom_call" | custom-call | tf_op jit(solution)/shard_map/pallas_call | solution.py:483

commit v5 on v4

--- a/solution.py
+++ b/solution.py
@@ -7,7 +7,7 @@
 from jax.sharding import PartitionSpec as P
 
 LANES = 128
-SIZES = (2, 4)
+SIZES = (1, 2, 3)
 BATCH = 4
 WIDE = 8
 MESH = pl.DeviceIdType.MESH
@@ -102,7 +102,7 @@
     n, nx, nu, tl, sl,
     a_hbm, k_hbm, ff_hbm, d_hbm, x0_hbm, x_tile, u_tile,
     a_ref, k_ref, ff_ref, d_ref, x0_ref,
-    leaf, nodes, pre, wf, tile, x_send, x_all, t_send, t_recv, p_send, m_recv, e_send, e_recv, send, recv,
+    leaf, nodes, pre, wf, w2, tile, x_send, x_all, t_send, t_recv, p_send, m_recv, e_send, e_recv, send, recv,
     in_sem, x_ssem, x_rsem, t_ssem, t_rsem, m_ssem, m_rsem, p_ssem, o_ssem, o_rsem,
 ):
     D = tile.shape[0]
@@ -306,6 +306,16 @@
             for t, value in zip(group, values):
                 wf[pl.ds(nx * tl + t, nu, stride=tl), :] = value
 
+    unit = 4 * LANES
+    ready = nx * tl // unit * unit
+
+    def halve(j, c):
+        part = pl.ds(pl.multiple_of(j * unit, unit), unit)
+        w2[part, :] = split(wf[part, :])
+        return c
+
+    lax.fori_loop(0, ready // unit, halve, 0)
+
     @pl.when(odd == 1)
     def _():
         x_wait(n - 1).wait_recv()
@@ -360,7 +370,7 @@
 
         for first in range(start, stop, 4 * LANES):
             here = slice(first, first + 4 * LANES)
-            part = apply_rows(stacked, split(wf[here, :]))
+            part = apply_rows(stacked, w2[here, :] if first < ready else split(wf[here, :]))
             for d in range(n):
                 send[d, :, here] = part[d * sl : (d + 1) * sl]
         recv[me, :, start:stop] = send[me, :, start:stop]
@@ -456,6 +466,7 @@
             pltpu.VMEM((tl, R, 2 * D), bf16),
             pltpu.VMEM((tl, R, 2 * D), bf16),
             pltpu.VMEM((rows * tl, D), f32),
+            pltpu.VMEM((rows * tl, 2 * D), bf16),
             pltpu.VMEM((D, D), f32),
             pltpu.VMEM((sl, D), f32),
             pltpu.VMEM((n, sl, D), f32),

time: 25.3 us -> 25.2 us (level)
  no operation moved by 1% of the time
where the time goes in v5:
time: 25.2 us; the launch traced here: 25 us
  Pallas kernels  24.3 us (96%)
  between operations  0.64 us (3%)
    pallas_call x1, Pallas kernels, body(): pl.pallas_call(functools.partial(rollout_kernel, n, nx, nu, tl, sl), out_...  23.3 us
    pallas_call x1, Pallas kernels, body(): pl.pallas_call(functools.partial(store_kernel, halves), out_shape=(jax.Sh...  1.04 us

profile of v5, /device:TPU:1, one launch (start us, length us, event | category | flops | bytes accessed | tf_op | source)
XLA Modules:
  0.0 25.0 jit_solution(5924905613199536545)
XLA Ops:
  0.6 23.3 %shard_map.68 = (f32[2,768,128]{2,1,0:T(8,128)S(1)}, f32[2,384,128]{2,1,0:T(8,128)S(1)}) custom-call(f32[32,96,96]{2,1,0:T(8,128)} %a_hbm.1, f32[32,48,96]{2,1,0:T(8,128)} %k_hbm.1, f32[32,48]{1,0:T(8,128)} %ff_hbm.1, f32[32,96]{1,0:T(8,128)} %d_hbm.1, f32[8,96]{1,0:T(8,128)} %bitcast.5), custom_call_target="tpu_custom_call" | custom-call | tf_op jit(solution)/shard_map/pallas_call | solution.py:451
  23.9 1.0 %shard_map.69 = (f32[8,96,256]{2,1,0:T(8,128)}, f32[8,48,256]{2,1,0:T(8,128)}) custom-call(f32[2,8,96,128]{3,2,1,0:T(8,128)S(1)} %bitcast.3, f32[2,8,48,128]{3,2,1,0:T(8,128)S(1)} %bitcast.4), custom_call_target="tpu_custom_call" | custom-call | tf_op jit(solution)/shard_map/pallas_call | solution.py:494
